TPU v7x, 128 devices: a whole 4x4x4 slice. The times are simulated.
128 devices in a mesh: row: 16 (over x_hi, y, core), col: 4 (over z), dp: 2 (over x_lo).
Axes of the slice: x: 4 (x_hi: 2, x_lo: 2; x = x_hi * 2 + x_lo), y: 4, z: 4, core: 2. Of those that a mesh axis runs over, the one named last changes fastest.
Arguments:
- slides: bfloat16 [2, 256, 128, 512], P('dp', 'row', 'col'), may hold values from -6 to 6
- cotangent: bfloat16 [2, 256, 128, 512], P('dp', 'row', 'col'), may hold values from -6 to 6
- kernel: float32 [2, 7, 7, 512], replicated, may hold values from -0.875 to 0.875
- kernel_bias: float32 [2, 512], replicated, may hold values from -3 to 3
- norm_gain: float32 [2, 512], replicated, may hold values from 0.1 to 1.9
- norm_bias: float32 [2, 512], replicated, may hold values from -3 to 3
- weight_in: bfloat16 [2, 512, 2048], P(None, 'dp'), may hold values from -0.25 to 0.25
- bias_in: float32 [2, 2048], replicated, may hold values from -3 to 3
- weight_out: bfloat16 [2, 2048, 512], P(None, None, 'dp'), may hold values from -0.125 to 0.125
- bias_out: float32 [2, 512], replicated, may hold values from -3 to 3
- layer_scale: float32 [2, 512], replicated, may hold values from 0.3 to 1.5
Outputs:
- output: bfloat16 [2, 256, 128, 512], P('dp', 'row', 'col')
- grad_slides: bfloat16 [2, 256, 128, 512], P('dp', 'row', 'col')
- grad_weight_in: float32 [2, 512, 2048], P(None, 'dp')
- grad_weight_out: float32 [2, 2048, 512], P(None, None, 'dp')
- grad_kernel: float32 [2, 7, 7, 512], replicated
- grad_channel: float32 [2, 5, 512], replicated
- grad_bias_in: float32 [2, 2048], replicated
All inputs are finite; a program needn't handle non-finite values.
Results may differ from a plain program's by a relative error of at most 0.01.
Values may be sent and summed in bfloat16 or wider, within the bound.
No kernel may reach another device: no remote copies, remote signals or barrier semaphores. Data moves between devices by JAX's collectives and lax.ppermute only.
A program may use at most 128 MiB of HBM per device.

v0:
```python
import jax
import jax.numpy as jnp
from jax import lax
from jax.sharding import PartitionSpec as P

COEF = 0.7978845608028654
CUBIC = 0.044715
EPSILON = 1e-06
SPACE = ("xh", "y", "z")
HALF = 1024


def chips_along_x(step):

    def target(pos):
        x = (pos + step) % 4
        return x

    return [(pos, target(pos)) for pos in range(4)]


def swapped(value, axis):
    return lax.ppermute(value, axis, [(0, 1), (1, 0)])


def fetch_weights(own_in, own_out):
    core = lax.axis_index("core")
    part = lax.axis_index("dp")
    send_in = lax.dynamic_slice_in_dim(own_in, core * 128, 128, 0)
    send_out = lax.dynamic_slice_in_dim(own_out, core * 1024, 1024, 0)
    got_in = lax.ppermute(send_in, ("xh", "dp"), chips_along_x(1))
    got_out = lax.ppermute(send_out, ("xh", "dp"), chips_along_x(-1))
    mate_in = swapped(got_in, "core")
    mate_out = swapped(got_out, "core")
    first = core == 0
    other_in = jnp.concatenate(
        [jnp.where(first, got_in, mate_in), jnp.where(first, mate_in, got_in)], 0
    )
    other_out = jnp.concatenate(
        [jnp.where(first, got_out, mate_out), jnp.where(first, mate_out, got_out)], 0
    )
    low = part == 0
    full_in = jnp.concatenate(
        [jnp.where(low, own_in, other_in), jnp.where(low, other_in, own_in)], 0
    )
    full_out = jnp.concatenate(
        [jnp.where(low, own_out, other_out), jnp.where(low, other_out, own_out)], 1
    )
    return (full_in, full_out)


def with_halo(block, sides, width):
    for axis, dim in sides:
        count = lax.axis_size(axis)
        forward = [(i, i + 1) for i in range(count - 1)]
        backward = [(target, source) for source, target in forward]
        low = lax.ppermute(
            lax.slice_in_dim(block, block.shape[dim] - width, None, axis=dim), axis, forward
        )
        high = lax.ppermute(lax.slice_in_dim(block, 0, width, axis=dim), axis, backward)
        block = jnp.concatenate([low, block, high], axis=dim)
    return block


def gelu_tanh(values):
    inner = COEF * (values + CUBIC * values * values * values)
    return 0.5 * values * (1.0 + jnp.tanh(inner))


def gelu_slope(values):
    tangent = jnp.tanh(COEF * (values + CUBIC * values * values * values))
    return 0.5 * (1.0 + tangent) + 0.5 * values * (1.0 - tangent * tangent) * COEF * (
        1.0 + 3.0 * CUBIC * values * values
    )


def depthwise(padded, taps):
    height = padded.shape[1] - 6
    width = padded.shape[2] - 6
    total = jnp.zeros((padded.shape[0], height, width, padded.shape[3]), jnp.float32)
    for row_tap in range(7):
        for col_tap in range(7):
            window = padded[:, row_tap : row_tap + height, col_tap : col_tap + width, :].astype(
                jnp.float32
            )
            total = total + window * taps[row_tap, col_tap]
    return total


def tap_grads(padded, upstream):
    height = upstream.shape[1]
    width = upstream.shape[2]
    rows_out = []
    for row_tap in range(7):
        line = []
        for col_tap in range(7):
            window = padded[:, row_tap : row_tap + height, col_tap : col_tap + width, :].astype(
                jnp.float32
            )
            line.append(jnp.sum(window * upstream, axis=(0, 1, 2)))
        rows_out.append(jnp.stack(line))
    return jnp.stack(rows_out)


def forward_layer(
    padded, current, taps, tap_bias, gain, shift, weight_in, bias_in, weight_out, bias_out, scale
):
    channels = current.shape[-1]
    mixed = (depthwise(padded, taps) + tap_bias).reshape(-1, channels)
    center = mixed - jnp.mean(mixed, -1, keepdims=True)
    rstd = lax.rsqrt(jnp.mean(center * center, -1, keepdims=True) + EPSILON)
    normed = center * rstd
    normal_low = (normed * gain + shift).astype(jnp.bfloat16)
    hidden = jnp.dot(normal_low, weight_in, preferred_element_type=jnp.float32) + bias_in
    activated = gelu_tanh(hidden).astype(jnp.bfloat16)
    branch = jnp.dot(activated, weight_out, preferred_element_type=jnp.float32) + bias_out
    result = current.reshape(-1, channels).astype(jnp.float32) + scale * branch
    result = result.astype(jnp.bfloat16).reshape(current.shape)
    return (result, (normed, rstd, normal_low, hidden, activated, branch))


def backward_layer(upstream, saved, gain, weight_in, weight_out, scale):
    normed, rstd, normal_low, hidden, activated, branch = saved
    contract_rows = (((0,), (0,)), ((), ()))
    contract_cols = (((1,), (1,)), ((), ()))
    grad_scale = jnp.sum(upstream * branch, 0)
    grad_branch = upstream * scale
    grad_bias_out = jnp.sum(grad_branch, 0)
    branch_low = grad_branch.astype(jnp.bfloat16)
    grad_weight_out = lax.dot_general(
        branch_low, activated, contract_rows, preferred_element_type=jnp.float32
    )
    grad_act = lax.dot_general(
        branch_low, weight_out, contract_cols, preferred_element_type=jnp.float32
    )
    grad_hidden = grad_act * gelu_slope(hidden)
    grad_bias_in = jnp.sum(grad_hidden, 0)
    hidden_low = grad_hidden.astype(jnp.bfloat16)
    grad_weight_in = lax.dot_general(
        normal_low, hidden_low, contract_rows, preferred_element_type=jnp.float32
    )
    grad_normal = lax.dot_general(
        hidden_low, weight_in, contract_cols, preferred_element_type=jnp.float32
    )
    grad_gain = jnp.sum(grad_normal * normed, 0)
    grad_shift = jnp.sum(grad_normal, 0)
    scaled = grad_normal * gain
    grad_mixed = rstd * (
        scaled
        - jnp.mean(scaled, -1, keepdims=True)
        - normed * jnp.mean(scaled * normed, -1, keepdims=True)
    )
    grad_tap_bias = jnp.sum(grad_mixed, 0)
    channel_grads = jnp.stack([grad_tap_bias, grad_gain, grad_shift, grad_bias_out, grad_scale])
    return (grad_mixed, grad_weight_in, grad_weight_out, grad_bias_in, channel_grads)


def reduce_weights(grad_in, grad_out):
    core = lax.axis_index("core")
    both = jnp.stack([grad_in, grad_out], 1).astype(jnp.bfloat16)
    keep = lax.dynamic_slice_in_dim(both, core * HALF, HALF, 2)
    give = lax.dynamic_slice_in_dim(both, (1 - core) * HALF, HALF, 2)
    pair = keep.astype(jnp.float32) + swapped(give, "core").astype(jnp.float32)
    pair = pair.astype(jnp.bfloat16).reshape(64, 8, 2, HALF)
    pieces = lax.all_to_all(pair, ("dp", *SPACE), 0, 0, tiled=True)
    mine = jnp.sum(pieces.astype(jnp.float32), 0).astype(jnp.bfloat16)
    copies = jnp.broadcast_to(mine, (32, *mine.shape))
    whole = lax.all_to_all(copies, SPACE, 0, 0, tiled=True).reshape(256, 2, HALF)
    mate = swapped(whole, "core")
    first = core == 0
    full = jnp.concatenate(
        [jnp.where(first, whole, mate), jnp.where(first, mate, whole)], 2
    ).astype(jnp.float32)
    return (full[:, 0], full[:, 1].T)


def reduce_small(parts):
    axes = ("xh", "y", "core", "z", "dp")
    lines = jnp.concatenate([p.reshape(-1) for p in parts])
    count = lines.shape[0]
    spare = -count % (128 * 128)
    lines = jnp.pad(lines, (0, spare)).astype(jnp.bfloat16).reshape(128, -1)
    pieces = lax.all_to_all(lines, axes, 0, 0, tiled=True)
    mine = jnp.sum(pieces.astype(jnp.float32), 0, keepdims=True)
    whole = lax.all_gather(mine, axes, axis=0, tiled=True).reshape(-1)
    outs = []
    start = 0
    for p in parts:
        outs.append(whole[start : start + p.size].reshape(p.shape))
        start += p.size
    return outs


def per_device(
    slides,
    cotangent,
    kernel,
    kernel_bias,
    norm_gain,
    norm_bias,
    weight_in,
    bias_in,
    weight_out,
    bias_out,
    layer_scale,
):
    layers = weight_in.shape[0]
    channels = slides.shape[-1]
    current = slides
    caches = []
    paddings = []
    fetched = []
    for which in range(layers):
        full_in, full_out = fetch_weights(weight_in[which], weight_out[which])
        fetched.append((full_in, full_out))
        padded = with_halo(current, ((("xh", "y", "core"), 1), ("z", 2)), 3)
        current, cache = forward_layer(
            padded,
            current,
            kernel[which],
            kernel_bias[which],
            norm_gain[which],
            norm_bias[which],
            full_in,
            bias_in[which],
            full_out,
            bias_out[which],
            layer_scale[which],
        )
        caches.append(cache)
        paddings.append(padded)
    upstream = cotangent.astype(jnp.float32).reshape(-1, channels)
    grads_in = [None] * layers
    grads_out = [None] * layers
    grads_kernel = [None] * layers
    grads_channel = [None] * layers
    grads_bias = [None] * layers
    for which in reversed(range(layers)):
        full_in, full_out = fetched[which]
        grad_mixed, grad_in, grad_out, grad_bias, channel_grads = backward_layer(
            upstream, caches[which], norm_gain[which], full_in, full_out, layer_scale[which]
        )
        shaped = grad_mixed.reshape(slides.shape)
        rim = with_halo(
            shaped.astype(jnp.bfloat16), ((("xh", "y", "core"), 1), ("z", 2)), 3
        ).astype(shaped.dtype)
        local_taps = tap_grads(paddings[which], shaped)
        back = depthwise(rim, kernel[which][::-1, ::-1])
        upstream = upstream + back.reshape(-1, channels)
        grads_in[which], grads_out[which] = reduce_weights(grad_in, grad_out)
        grads_kernel[which], grads_channel[which], grads_bias[which] = (
            local_taps,
            channel_grads,
            grad_bias,
        )
    grad_slides = upstream.astype(jnp.bfloat16).reshape(slides.shape)
    small = reduce_small([jnp.stack(grads_kernel), jnp.stack(grads_channel), jnp.stack(grads_bias)])
    return (current, grad_slides, jnp.stack(grads_in), jnp.stack(grads_out), *small)


def solution(mesh):
    fine = jax.sharding.Mesh(mesh.devices.reshape(2, 4, 2, 4, 2), ("xh", "y", "core", "z", "dp"))
    rows = ("xh", "y", "core")
    return jax.shard_map(
        per_device,
        mesh=fine,
        in_specs=(
            P("dp", rows, "z", None),
            P("dp", rows, "z", None),
            P(),
            P(),
            P(),
            P(),
            P(None, "dp", None),
            P(),
            P(None, None, "dp"),
            P(),
            P(),
        ),
        out_specs=(
            P("dp", rows, "z", None),
            P("dp", rows, "z", None),
            P(None, "dp", None),
            P(None, None, "dp"),
            P(),
            P(),
            P(),
        ),
        check_vma=False,
    )
```

profile of v0, /device:TPU:1, one launch (start us, length us, event | category | flops | bytes accessed | tf_op | source)
XLA Modules:
  0.0 720.8 jit_solution(1753578063245275340)
XLA Ops:
  0.6 2.8 fusion.397
  3.5 1.9 dynamic-slice_bitcast_fusion
  5.4 3.3 collective-permute-start.14
  11.6 4.3 collective-permute-start
  16.0 1.9 collective-permute-start.1
  19.4 2.0 dynamic-slice_bitcast_fusion.1
  26.2 1.9 dynamic-slice_bitcast_fusion.3
  34.6 4.2 collective-permute-start.2
  41.0 15.6 %fusion.394 = (f32[16,32]{1,0:T(8,128)S(1)}, f32[1,16,32,512]{3,2,1,0:T(8,128)S(1)}) fusion(f32[512]{0:T(512)} %bitcast.599, f32[512]{0:T(512)S(1)} %bitcast.396, bf16[1,22,3,512]{3,2,1,0:T(4,128)(2,1)} %copy-done.36, bf16[1,22,32,512]{3,2,1,0:T(8,128)(2,1)S(1)} %get-tuple-element.321, f32[512]{0:T(512)S(1)} %bitcast.398, f32[512]{0:T(512)S(1)} %bitcast.400, ...), kind=kLoop, calls=%fused_computation.914 | loop fusion | flops 71826944 | bytes 5679104 | tf_op jit(solution)/shard_map/reduce_sum | solution.py:110
  56.6 3.1 collective-permute-start.13
  65.3 2.5 bitcast_select_fusion.3
  72.2 2.3 bitcast_select_fusion.1
  74.5 2.6 fusion.327
  77.3 2.3 collective-permute-start.9
  79.6 3.3 collective-permute-start.8
  84.6 3.6 collective-permute-start.10
  88.2 1.8 collective-permute-start.11
  90.7 3.0 collective-permute-done.11
  95.5 11.4 %fusion.392 = (f32[16,32]{1,0:T(8,128)S(1)}, f32[1,16,32,512]{3,2,1,0:T(8,128)}) fusion(f32[512]{0:T(512)} %bitcast.604, f32[512]{0:T(512)S(1)} %bitcast.494, bf16[1,22,35,512]{3,2,1,0:T(8,128)(2,1)S(1)} %get-tuple-element.200, f32[512]{0:T(512)S(1)} %bitcast.497, f32[512]{0:T(512)S(1)} %bitcast.499, f32[512]{0:T(512)S(1)} %bitcast.501, ...), kind=kLoop, calls=%fused_computation.913 | loop fusion | flops 40369664 | bytes 23894016 | tf_op jit(solution)/shard_map/reduce_sum | solution.py:110
  110.2 2.8 fusion.24
  113.1 4.2 fusion.416
  117.3 2.1 multiply_reduce_fusion
  120.7 2.0 fusion.15
  122.8 4.3 fusion.223
  127.1 3.4 fusion.219
  131.2 1.9 collective-permute-start.17
  133.1 5.6 collective-permute-start.16
  140.3 2.2 fusion.220
  154.4 4.2 collective-permute-start.18
  184.8 10.3 %multiply_reduce_fusion.2 = (bf16[512]{0:T(512)(128)(2,1)}, bf16[512]{0:T(512)(128)(2,1)S(1)}, f32[1,16,32,512]{3,2,1,0:T(8,128)S(1)}) fusion(bf16[1,16,32,512]{3,2,1,0:T(8,128)(2,1)} %param.12, f32[512]{0:T(512)} %bitcast.601, f32[512]{0:T(512)} %bitcast.591, f32[512]{0:T(512)S(1)} %bitcast.493, f32[1,22,38,512]{3,2,1,0:T(8,128)S(1)} %maximum_convert_fusion.2, ...), kind=kLoop, calls=%fused_computation.716 | loop fusion | flops 26999808 | bytes 53059584 | tf_op jit(solution)/shard_map/reduce_sum | solution.py:128
  195.2 3.4 multiply_reduce_fusion.1
  198.8 3.6 fusion.417
  202.4 2.1 multiply_reduce_fusion.3
  205.8 2.0 fusion.13
  217.8 3.7 fusion.121
  221.6 2.9 fusion.123
  224.6 2.0 fusion.125
  226.8 1.9 fusion.120
  228.7 2.2 fusion.124
  234.5 14.5 %all-to-all-start.4 = ((bf16[128,2,256]{2,1,0:T(2,128)(2,1)}), bf16[128,2,256]{2,1,0:T(2,128)(2,1)S(1)}, u32[]{:S(2)}, u32[]{:S(2)}) async-start(bf16[128,2,256]{2,1,0:T(2,128)(2,1)} %reshape.941), calls=%async_computation.4 | async-start | bytes 262144 | tf_op jit(solution)/shard_map/all_to_all | solution.py:183
  249.1 3.1 fusion.17
  253.8 5.1 all-to-all-done.4
  258.9 5.7 all-to-all-start.2
  264.6 3.1 fusion.16
  269.3 22.3 %all-to-all-done.2 = bf16[64,8,2,1024]{3,1,2,0:T(8,128)(2,1)} async-done(((bf16[64,8,2,1024]{3,1,2,0:T(8,128)(2,1)}), bf16[64,8,2,1024]{3,1,2,0:T(8,128)(2,1)}, u32[]{:S(2)}, u32[]{:S(2)}) %all-to-all-start.2) | async-done | bytes 2097184 | tf_op jit(solution)/shard_map/all_to_all | solution.py:165
  291.7 8.1 %all-to-all-start = ((bf16[64,8,2,1024]{3,1,2,0:T(8,128)(2,1)}), bf16[64,8,2,1024]{3,1,2,0:T(8,128)(2,1)}, u32[]{:S(2)}, u32[]{:S(2)}) async-start(bf16[64,8,2,1024]{3,1,2,0:T(8,128)(2,1)} %copy.26), calls=%async_computation | async-start | bytes 4194304 | tf_op jit(solution)/shard_map/all_to_all | solution.py:165
  299.7 2.0 reduce_sum.1104
  301.7 23.7 %all-to-all-done = bf16[64,8,2,1024]{3,1,2,0:T(8,128)(2,1)} async-done(((bf16[64,8,2,1024]{3,1,2,0:T(8,128)(2,1)}), bf16[64,8,2,1024]{3,1,2,0:T(8,128)(2,1)}, u32[]{:S(2)}, u32[]{:S(2)}) %all-to-all-start) | async-done | bytes 2097184 | tf_op jit(solution)/shard_map/all_to_all | solution.py:165
  326.4 8.3 %all-to-all-start.3 = ((bf16[32,8,2,1024]{3,1,2,0:T(8,128)(2,1)}), bf16[32,8,2,1024]{3,1,2,0:T(8,128)(2,1)S(1)}, u32[]{:S(2)}, u32[]{:S(2)}) async-start(bf16[32,8,2,1024]{3,1,2,0:T(8,128)(2,1)} %broadcast_in_dim.7), calls=%async_computation.3 | async-start | bytes 2097152 | tf_op jit(solution)/shard_map/all_to_all | solution.py:168
  334.9 2.1 reduce_sum.1103
  337.0 13.3 %all-to-all-done.3 = bf16[32,8,2,1024]{3,1,2,0:T(8,128)(2,1)S(1)} async-done(((bf16[32,8,2,1024]{3,1,2,0:T(8,128)(2,1)}), bf16[32,8,2,1024]{3,1,2,0:T(8,128)(2,1)S(1)}, u32[]{:S(2)}, u32[]{:S(2)}) %all-to-all-start.3) | async-done | bytes 1048608 | tf_op jit(solution)/shard_map/all_to_all | solution.py:168
  351.4 6.2 all-to-all-start.1
  357.6 4.2 collective-permute-start.21
  361.8 3.2 collective-permute-start.20
  365.1 6.7 collective-permute-done.21
  373.2 4.0 collective-permute-start.22
  377.6 293.8 %all-gather.1 = f32[128,1,512]{2,1,0:T(1,128)S(1)} all-gather(f32[1,1,512]{2,1,0:T(1,128)S(1)} %bitcast.600), channel_id=2, replica_groups=mesh['xh'=2,'y'=4,'core'=2,'z'=4,'dp'=2] {'xh','y','core','z','dp'}, dimensions={0}, use_global_device_ids=true | all-gather | bytes 264192 | tf_op jit(solution)/shard_map/all_gather | solution.py:185
  676.6 16.4 %collective-permute-start.27 = (bf16[256,2,1024]{2,0,1:T(8,128)(2,1)}, bf16[256,2,1024]{2,0,1:T(8,128)(2,1)}, u32[]{:S(2)}, u32[]{:S(2)}) collective-permute-start(bf16[256,2,1024]{2,0,1:T(8,128)(2,1)} %bitcast.371), channel_id=1, source_target_pairs={{0,8},{8,0},{1,9},{9,1},{2,10},{10,2},{3,11},{11,3},{4,12},{12,4},... | collective-permute-start | bytes 3145736 | tf_op jit(solution)/shard_map/ppermute | solution.py:23
  694.5 9.4 %fusion.226 = bf16[1,16,32,512]{3,2,1,0:T(8,128)(2,1)} fusion(f32[1,22,38,512]{3,2,1,0:T(8,128)S(1)} %maximum_convert_fusion.3, f32[1,16,32,512]{3,2,1,0:T(8,128)} %copy-done.23, bf16[1,16,32,512]{3,2,1,0:T(8,128)(2,1)} %param.12, f32[512]{0:T(512)S(1)} %bitcast.397, f32[512]{0:T(512)S(1)} %bitcast.399, f32[512]{0:T(512)S(1)} %bitcast.401, ...), kind=kLoop, calls=%fused_computation.493 | loop fusion | flops 26476544 | bytes 53577728 | tf_op jit(solution)/shard_map/convert_element_type | solution.py:256
  703.9 1.8 broadcast_select_fusion.1
  707.3 1.7 slice_bitcast_fusion.1
  709.0 2.3 pad_maximum_fusion.1
  711.3 5.3 copy.31
  716.7 4.0 pad_maximum_fusion
  (485 shorter events, 106.5 us)
Async XLA Ops:
  3.4 18.8 %copy-start.51 = (f32[2,7,7,512]{3,0,2,1:T(2,128)S(1)}, f32[2,7,7,512]{3,0,2,1:T(2,128)}, u32[]{:S(2)}) copy-start(f32[2,7,7,512]{3,0,2,1:T(2,128)} %param.13) | copy-start | bytes 602116
  3.4 21.0 %copy-start.100 = (f32[2,512]{1,0:T(2,128)S(1)}, f32[2,512]{1,0:T(2,128)}, u32[]{:S(2)}) copy-start(f32[2,512]{1,0:T(2,128)} %param.21) | copy-start | bytes 12292
  3.4 21.6 %copy-start.101 = (f32[2,512]{1,0:T(2,128)S(1)}, f32[2,512]{1,0:T(2,128)}, u32[]{:S(2)}) copy-start(f32[2,512]{1,0:T(2,128)} %param.20) | copy-start | bytes 12292
  3.4 22.2 %copy-start.102 = (f32[2,512]{1,0:T(2,128)S(1)}, f32[2,512]{1,0:T(2,128)}, u32[]{:S(2)}) copy-start(f32[2,512]{1,0:T(2,128)} %param.14) | copy-start | bytes 12292
  5.4 56.6 %collective-permute-start.14 = (bf16[1024,256]{1,0:T(8,128)(2,1)}, bf16[1024,256]{1,0:T(8,128)(2,1)}, u32[]{:S(2)}, u32[]{:S(2)}) collective-permute-start(bf16[1024,256]{1,0:T(8,128)(2,1)} %dynamic-slice_bitcast_fusion), channel_id=1, source_target_pairs={{0,65},{1,0},{64,1},{65,64},{2,67},{3,2},{66,3},{67,66},{4,69},{5,... | collective-permute-start | bytes 1572872 | tf_op jit(solution)/shard_map/ppermute | solution.py:32
  8.7 19.4 %copy-start.83 = (f32[2,2048]{1,0:T(2,128)S(1)}, f32[2,2048]{1,0:T(2,128)}, u32[]{:S(2)}) copy-start(f32[2,2048]{1,0:T(2,128)} %param.18) | copy-start | bytes 49156
  9.5 20.0 %copy-start.21 = (bf16[1,16,32,512]{3,2,1,0:T(8,128)(2,1)S(1)}, bf16[1,16,32,512]{3,2,1,0:T(8,128)(2,1)}, u32[]{:S(2)}) copy-start(bf16[1,16,32,512]{3,2,1,0:T(8,128)(2,1)} %param.12) | copy-start | bytes 1572868
  9.5 53.0 %collective-permute-start.6 = (bf16[1024,256]{1,0:T(8,128)(2,1)}, bf16[1024,256]{1,0:T(8,128)(2,1)}, u32[]{:S(2)}, u32[]{:S(2)}) collective-permute-start(bf16[1024,256]{1,0:T(8,128)(2,1)} %dynamic-slice_bitcast_fusion.2), channel_id=1, source_target_pairs={{0,65},{1,0},{64,1},{65,64},{2,67},{3,2},{66,3},{67,66},{4,69},{5,... | collective-permute-start | bytes 1572872 | tf_op jit(solution)/shard_map/ppermute | solution.py:32
  11.6 19.3 %collective-permute-start = (bf16[1,3,32,512]{3,2,1,0:T(8,128)(2,1)S(1)}, bf16[1,3,32,512]{3,2,1,0:T(8,128)(2,1)S(1)}, u32[]{:S(2)}, u32[]{:S(2)}) collective-permute-start(bf16[1,3,32,512]{3,2,1,0:T(8,128)(2,1)S(1)} %get-tuple-element.217), channel_id=1, source_target_pairs={{0,8},{8,16},{16,24},{24,32},{32,40},{40,48},{48,56},{56,64},{64,7... | collective-permute-start | bytes 294920 | tf_op jit(solution)/shard_map/ppermute | solution.py:57
  16.0 16.2 %collective-permute-start.1 = (bf16[1,3,32,512]{3,2,1,0:T(8,128)(2,1)}, bf16[1,3,32,512]{3,2,1,0:T(8,128)(2,1)}, u32[]{:S(2)}, u32[]{:S(2)}) collective-permute-start(bf16[1,3,32,512]{3,2,1,0:T(8,128)(2,1)} %get-tuple-element.216), channel_id=1, source_target_pairs={{8,0},{16,8},{24,16},{32,24},{40,32},{48,40},{56,48},{64,56},{72,6... | collective-permute-start | bytes 294920 | tf_op jit(solution)/shard_map/ppermute | solution.py:60
  19.4 19.4 %copy-start.104 = (f32[2,512]{1,0:T(2,128)S(1)}, f32[2,512]{1,0:T(2,128)}, u32[]{:S(2)}) copy-start(f32[2,512]{1,0:T(2,128)} %param.15) | copy-start | bytes 12292
  19.4 21.6 %copy-start.17 = (bf16[1,16,32,512]{3,2,1,0:T(8,128)(2,1)S(1)}, bf16[1,16,32,512]{3,2,1,0:T(8,128)(2,1)}, u32[]{:S(2)}) copy-start(bf16[1,16,32,512]{3,2,1,0:T(8,128)(2,1)} %param.11) | copy-start | bytes 1572868
  21.3 35.3 %collective-permute-start.12 = (bf16[128,2048]{1,0:T(8,128)(2,1)}, bf16[128,2048]{1,0:T(8,128)(2,1)}, u32[]{:S(2)}, u32[]{:S(2)}) collective-permute-start(bf16[128,2048]{1,0:T(8,128)(2,1)} %dynamic-slice_bitcast_fusion.1), channel_id=1, source_target_pairs={{0,1},{1,64},{64,65},{65,0},{2,3},{3,66},{66,67},{67,2},{4,5},{5,6... | collective-permute-start | bytes 1572872 | tf_op jit(solution)/shard_map/ppermute | solution.py:31
  23.1 33.5 %copy-start.56 = (f32[1,1,512]{2,1,0:T(1,128)}, f32[1,1,512]{2,1,0:T(1,128)S(1)}, u32[]{:S(2)}) copy-start(f32[1,1,512]{2,1,0:T(1,128)S(1)} %get-tuple-element.269) | copy-start | bytes 6148
  23.1 33.5 %copy-start.58 = (f32[1,1,512]{2,1,0:T(1,128)}, f32[1,1,512]{2,1,0:T(1,128)S(1)}, u32[]{:S(2)}) copy-start(f32[1,1,512]{2,1,0:T(1,128)S(1)} %get-tuple-element.270) | copy-start | bytes 6148
  23.1 33.5 %copy-start.60 = (f32[1,1,512]{2,1,0:T(1,128)}, f32[1,1,512]{2,1,0:T(1,128)S(1)}, u32[]{:S(2)}) copy-start(f32[1,1,512]{2,1,0:T(1,128)S(1)} %get-tuple-element.271) | copy-start | bytes 6148
  23.1 33.5 %copy-start.62 = (f32[1,1,512]{2,1,0:T(1,128)}, f32[1,1,512]{2,1,0:T(1,128)S(1)}, u32[]{:S(2)}) copy-start(f32[1,1,512]{2,1,0:T(1,128)S(1)} %get-tuple-element.272) | copy-start | bytes 6148
  32.2 29.8 %copy-start = (bf16[1,19,32,512]{3,2,1,0:T(8,128)(2,1)}, bf16[1,19,32,512]{3,2,1,0:T(8,128)(2,1)S(1)}, u32[]{:S(2)}) copy-start(bf16[1,19,32,512]{3,2,1,0:T(8,128)(2,1)S(1)} %get-tuple-element.213) | copy-start | bytes 1867780
  33.3 6.1 collective-permute-start.3
  34.6 5.7 collective-permute-start.2
  39.4 21.4 %collective-permute-start.4 = (bf16[128,2048]{1,0:T(8,128)(2,1)}, bf16[128,2048]{1,0:T(8,128)(2,1)}, u32[]{:S(2)}, u32[]{:S(2)}) collective-permute-start(bf16[128,2048]{1,0:T(8,128)(2,1)} %dynamic-slice_bitcast_fusion.3), channel_id=1, source_target_pairs={{0,1},{1,64},{64,65},{65,0},{2,3},{3,66},{66,67},{67,2},{4,5},{5,6... | collective-permute-start | bytes 1572872 | tf_op jit(solution)/shard_map/ppermute | solution.py:31
  56.6 6.3 collective-permute-start.13
  60.8 3.4 collective-permute-start.5
  62.0 5.9 collective-permute-start.15
  62.5 8.2 %collective-permute-start.7 = (bf16[1024,256]{1,0:T(8,128)(2,1)}, bf16[1024,256]{1,0:T(8,128)(2,1)S(1)}, u32[]{:S(2)}, u32[]{:S(2)}) collective-permute-start(bf16[1024,256]{1,0:T(8,128)(2,1)} %collective-permute-done.6), channel_id=1, source_target_pairs={{0,8},{8,0},{1,9},{9,1},{2,10},{10,2},{3,11},{11,3},{4,12},{12,4},... | collective-permute-start | bytes 1572872 | tf_op jit(solution)/shard_map/ppermute | solution.py:23
  77.2 18.2 %copy-start.71 = (f32[1,1,512]{2,1,0:T(1,128)S(1)}, f32[1,1,512]{2,1,0:T(1,128)}, u32[]{:S(2)}) copy-start(f32[1,1,512]{2,1,0:T(1,128)} %get-tuple-element.220) | copy-start | bytes 6148
  77.2 18.2 %copy-start.72 = (f32[1,1,512]{2,1,0:T(1,128)S(1)}, f32[1,1,512]{2,1,0:T(1,128)}, u32[]{:S(2)}) copy-start(f32[1,1,512]{2,1,0:T(1,128)} %get-tuple-element.221) | copy-start | bytes 6148
  77.2 18.2 %copy-start.73 = (f32[1,1,512]{2,1,0:T(1,128)S(1)}, f32[1,1,512]{2,1,0:T(1,128)}, u32[]{:S(2)}) copy-start(f32[1,1,512]{2,1,0:T(1,128)} %get-tuple-element.222) | copy-start | bytes 6148
  77.2 18.2 %copy-start.74 = (f32[1,1,512]{2,1,0:T(1,128)S(1)}, f32[1,1,512]{2,1,0:T(1,128)}, u32[]{:S(2)}) copy-start(f32[1,1,512]{2,1,0:T(1,128)} %get-tuple-element.223) | copy-start | bytes 6148
  77.2 18.2 %copy-start.75 = (f32[1,1,512]{2,1,0:T(1,128)S(1)}, f32[1,1,512]{2,1,0:T(1,128)}, u32[]{:S(2)}) copy-start(f32[1,1,512]{2,1,0:T(1,128)} %get-tuple-element.224) | copy-start | bytes 6148
  77.2 18.2 %copy-start.76 = (f32[1,1,512]{2,1,0:T(1,128)S(1)}, f32[1,1,512]{2,1,0:T(1,128)}, u32[]{:S(2)}) copy-start(f32[1,1,512]{2,1,0:T(1,128)} %get-tuple-element.225) | copy-start | bytes 6148
  77.3 18.2 %copy-start.77 = (f32[1,1,512]{2,1,0:T(1,128)S(1)}, f32[1,1,512]{2,1,0:T(1,128)}, u32[]{:S(2)}) copy-start(f32[1,1,512]{2,1,0:T(1,128)} %get-tuple-element.226) | copy-start | bytes 6148
  77.3 18.2 %copy-start.78 = (f32[1,1,512]{2,1,0:T(1,128)S(1)}, f32[1,1,512]{2,1,0:T(1,128)}, u32[]{:S(2)}) copy-start(f32[1,1,512]{2,1,0:T(1,128)} %get-tuple-element.227) | copy-start | bytes 6148
  77.3 6.3 collective-permute-start.9
  79.6 4.9 collective-permute-start.8
  84.6 6.1 collective-permute-start.10
  88.2 5.5 collective-permute-start.11
  131.2 20.8 %collective-permute-start.17 = (bf16[1,3,32,512]{3,2,1,0:T(8,128)(2,1)}, bf16[1,3,32,512]{3,2,1,0:T(8,128)(2,1)S(1)}, u32[]{:S(2)}, u32[]{:S(2)}) collective-permute-start(bf16[1,3,32,512]{3,2,1,0:T(8,128)(2,1)} %get-tuple-element.210), channel_id=1, source_target_pairs={{8,0},{16,8},{24,16},{32,24},{40,32},{48,40},{56,48},{64,56},{72,6... | collective-permute-start | bytes 294920 | tf_op jit(solution)/shard_map/ppermute | solution.py:60
  133.1 18.9 %collective-permute-start.16 = (bf16[1,3,32,512]{3,2,1,0:T(8,128)(2,1)}, bf16[1,3,32,512]{3,2,1,0:T(8,128)(2,1)S(1)}, u32[]{:S(2)}, u32[]{:S(2)}) collective-permute-start(bf16[1,3,32,512]{3,2,1,0:T(8,128)(2,1)} %get-tuple-element.209), channel_id=1, source_target_pairs={{0,8},{8,16},{16,24},{24,32},{32,40},{40,48},{48,56},{56,64},{64,7... | collective-permute-start | bytes 294920 | tf_op jit(solution)/shard_map/ppermute | solution.py:57
  140.3 108.7 %collective-permute-start.26 = (bf16[512,2,1024]{2,0,1:T(8,128)(2,1)}, bf16[512,2,1024]{2,0,1:T(8,128)(2,1)}, u32[]{:S(2)}, u32[]{:S(2)}) collective-permute-start(bf16[512,2,1024]{2,0,1:T(8,128)(2,1)} %fusion.18), channel_id=1, source_target_pairs={{0,8},{8,0},{1,9},{9,1},{2,10},{10,2},{3,11},{11,3},{4,12},{12,4},... | collective-permute-start | bytes 6291464 | tf_op jit(solution)/shard_map/ppermute | solution.py:23
  153.1 30.2 %collective-permute-start.19 = (bf16[1,22,3,512]{3,2,1,0:T(4,128)(2,1)S(1)}, bf16[1,22,3,512]{3,2,1,0:T(4,128)(2,1)S(1)}, u32[]{:S(2)}, u32[]{:S(2)}) collective-permute-start(bf16[1,22,3,512]{3,2,1,0:T(4,128)(2,1)S(1)} %get-tuple-element.198), channel_id=1, source_target_pairs={{2,0},{4,2},{6,4},{3,1},{5,3},{7,5},{10,8},{12,10},{14,12},{11,9},... | collective-permute-start | bytes 202760 | tf_op jit(solution)/shard_map/ppermute | solution.py:60
  154.4 28.9 %collective-permute-start.18 = (bf16[1,22,3,512]{3,2,1,0:T(4,128)(2,1)S(1)}, bf16[1,22,3,512]{3,2,1,0:T(4,128)(2,1)S(1)}, u32[]{:S(2)}, u32[]{:S(2)}) collective-permute-start(bf16[1,22,3,512]{3,2,1,0:T(4,128)(2,1)S(1)} %get-tuple-element.197), channel_id=1, source_target_pairs={{0,2},{2,4},{4,6},{1,3},{3,5},{5,7},{8,10},{10,12},{12,14},{9,11},... | collective-permute-start | bytes 202760 | tf_op jit(solution)/shard_map/ppermute | solution.py:57
  158.5 36.6 %copy-start.52 = (bf16[7,7,512]{2,1,0:T(8,128)(2,1)}, bf16[7,7,512]{2,1,0:T(8,128)(2,1)S(1)}, u32[]{:S(2)}) copy-start(bf16[7,7,512]{2,1,0:T(8,128)(2,1)S(1)} %constant_dynamic-update-slice_fusion.18) | copy-start | bytes 150532
  209.6 55.0 %collective-permute-start.24 = (bf16[512,2,1024]{2,0,1:T(8,128)(2,1)}, bf16[512,2,1024]{2,0,1:T(8,128)(2,1)}, u32[]{:S(2)}, u32[]{:S(2)}) collective-permute-start(bf16[512,2,1024]{2,0,1:T(8,128)(2,1)} %fusion.20), channel_id=1, source_target_pairs={{0,8},{8,0},{1,9},{9,1},{2,10},{10,2},{3,11},{11,3},{4,12},{12,4},... | collective-permute-start | bytes 6291464 | tf_op jit(solution)/shard_map/ppermute | solution.py:23
  234.5 24.4 %all-to-all-start.4 = ((bf16[128,2,256]{2,1,0:T(2,128)(2,1)}), bf16[128,2,256]{2,1,0:T(2,128)(2,1)S(1)}, u32[]{:S(2)}, u32[]{:S(2)}) async-start(bf16[128,2,256]{2,1,0:T(2,128)(2,1)} %reshape.941), calls=%async_computation.4 | async-start | bytes 262144 | tf_op jit(solution)/shard_map/all_to_all | solution.py:183
  258.9 32.8 %all-to-all-start.2 = ((bf16[64,8,2,1024]{3,1,2,0:T(8,128)(2,1)}), bf16[64,8,2,1024]{3,1,2,0:T(8,128)(2,1)}, u32[]{:S(2)}, u32[]{:S(2)}) async-start(bf16[64,8,2,1024]{3,1,2,0:T(8,128)(2,1)} %copy.28), calls=%async_computation.2 | async-start | bytes 4194304 | tf_op jit(solution)/shard_map/all_to_all | solution.py:165
  291.7 33.7 %all-to-all-start = ((bf16[64,8,2,1024]{3,1,2,0:T(8,128)(2,1)}), bf16[64,8,2,1024]{3,1,2,0:T(8,128)(2,1)}, u32[]{:S(2)}, u32[]{:S(2)}) async-start(bf16[64,8,2,1024]{3,1,2,0:T(8,128)(2,1)} %copy.26), calls=%async_computation | async-start | bytes 4194304 | tf_op jit(solution)/shard_map/all_to_all | solution.py:165
  326.4 23.8 %all-to-all-start.3 = ((bf16[32,8,2,1024]{3,1,2,0:T(8,128)(2,1)}), bf16[32,8,2,1024]{3,1,2,0:T(8,128)(2,1)S(1)}, u32[]{:S(2)}, u32[]{:S(2)}) async-start(bf16[32,8,2,1024]{3,1,2,0:T(8,128)(2,1)} %broadcast_in_dim.7), calls=%async_computation.3 | async-start | bytes 2097152 | tf_op jit(solution)/shard_map/all_to_all | solution.py:168
  334.9 337.1 %copy-start.20 = (bf16[1,16,32,512]{3,2,1,0:T(8,128)(2,1)}, bf16[1,16,32,512]{3,2,1,0:T(8,128)(2,1)S(1)}, u32[]{:S(2)}) copy-start(bf16[1,16,32,512]{3,2,1,0:T(8,128)(2,1)S(1)} %convert_element_type.643) | copy-start | bytes 1572868
  351.4 341.6 %all-to-all-start.1 = ((bf16[32,8,2,1024]{3,1,2,0:T(8,128)(2,1)}), bf16[32,8,2,1024]{3,1,2,0:T(8,128)(2,1)}, u32[]{:S(2)}, u32[]{:S(2)}) async-start(bf16[32,8,2,1024]{3,1,2,0:T(8,128)(2,1)} %broadcast_in_dim.6), calls=%async_computation.1 | async-start | bytes 2097152 | tf_op jit(solution)/shard_map/all_to_all | solution.py:168
  357.6 14.2 %collective-permute-start.21 = (bf16[1,3,32,512]{3,2,1,0:T(8,128)(2,1)S(1)}, bf16[1,3,32,512]{3,2,1,0:T(8,128)(2,1)S(1)}, u32[]{:S(2)}, u32[]{:S(2)}) collective-permute-start(bf16[1,3,32,512]{3,2,1,0:T(8,128)(2,1)S(1)} %get-tuple-element.208), channel_id=1, source_target_pairs={{8,0},{16,8},{24,16},{32,24},{40,32},{48,40},{56,48},{64,56},{72,6... | collective-permute-start | bytes 294920 | tf_op jit(solution)/shard_map/ppermute | solution.py:60
  361.8 10.0 %collective-permute-start.20 = (bf16[1,3,32,512]{3,2,1,0:T(8,128)(2,1)S(1)}, bf16[1,3,32,512]{3,2,1,0:T(8,128)(2,1)S(1)}, u32[]{:S(2)}, u32[]{:S(2)}) collective-permute-start(bf16[1,3,32,512]{3,2,1,0:T(8,128)(2,1)S(1)} %get-tuple-element.207), channel_id=1, source_target_pairs={{0,8},{8,16},{16,24},{24,32},{32,40},{40,48},{48,56},{56,64},{64,7... | collective-permute-start | bytes 294920 | tf_op jit(solution)/shard_map/ppermute | solution.py:57
  371.9 302.3 %collective-permute-start.23 = (bf16[1,22,3,512]{3,2,1,0:T(4,128)(2,1)S(1)}, bf16[1,22,3,512]{3,2,1,0:T(4,128)(2,1)S(1)}, u32[]{:S(2)}, u32[]{:S(2)}) collective-permute-start(bf16[1,22,3,512]{3,2,1,0:T(4,128)(2,1)S(1)} %get-tuple-element.196), channel_id=1, source_target_pairs={{2,0},{4,2},{6,4},{3,1},{5,3},{7,5},{10,8},{12,10},{14,12},{11,9},... | collective-permute-start | bytes 202760 | tf_op jit(solution)/shard_map/ppermute | solution.py:60
  373.2 301.0 %collective-permute-start.22 = (bf16[1,22,3,512]{3,2,1,0:T(4,128)(2,1)S(1)}, bf16[1,22,3,512]{3,2,1,0:T(4,128)(2,1)S(1)}, u32[]{:S(2)}, u32[]{:S(2)}) collective-permute-start(bf16[1,22,3,512]{3,2,1,0:T(4,128)(2,1)S(1)} %get-tuple-element.195), channel_id=1, source_target_pairs={{0,2},{2,4},{4,6},{1,3},{3,5},{5,7},{8,10},{10,12},{12,14},{9,11},... | collective-permute-start | bytes 202760 | tf_op jit(solution)/shard_map/ppermute | solution.py:57
  671.4 23.0 %copy-start.57 = (f32[1,1,512]{2,1,0:T(1,128)S(1)}, f32[1,1,512]{2,1,0:T(1,128)}, u32[]{:S(2)}) copy-start(f32[1,1,512]{2,1,0:T(1,128)} %copy-done.56) | copy-start | bytes 6148
  671.4 23.0 %copy-start.59 = (f32[1,1,512]{2,1,0:T(1,128)S(1)}, f32[1,1,512]{2,1,0:T(1,128)}, u32[]{:S(2)}) copy-start(f32[1,1,512]{2,1,0:T(1,128)} %copy-done.58) | copy-start | bytes 6148
  671.4 23.0 %copy-start.61 = (f32[1,1,512]{2,1,0:T(1,128)S(1)}, f32[1,1,512]{2,1,0:T(1,128)}, u32[]{:S(2)}) copy-start(f32[1,1,512]{2,1,0:T(1,128)} %copy-done.60) | copy-start | bytes 6148
  671.4 23.0 %copy-start.63 = (f32[1,1,512]{2,1,0:T(1,128)S(1)}, f32[1,1,512]{2,1,0:T(1,128)}, u32[]{:S(2)}) copy-start(f32[1,1,512]{2,1,0:T(1,128)} %copy-done.62) | copy-start | bytes 6148
  671.4 23.0 %copy-start.64 = (f32[1,1,512]{2,1,0:T(1,128)S(1)}, f32[1,1,512]{2,1,0:T(1,128)}, u32[]{:S(2)}) copy-start(f32[1,1,512]{2,1,0:T(1,128)} %get-tuple-element.273) | copy-start | bytes 6148
  671.4 23.0 %copy-start.65 = (f32[1,1,512]{2,1,0:T(1,128)S(1)}, f32[1,1,512]{2,1,0:T(1,128)}, u32[]{:S(2)}) copy-start(f32[1,1,512]{2,1,0:T(1,128)} %get-tuple-element.274) | copy-start | bytes 6148
  671.4 23.0 %copy-start.66 = (f32[1,1,512]{2,1,0:T(1,128)S(1)}, f32[1,1,512]{2,1,0:T(1,128)}, u32[]{:S(2)}) copy-start(f32[1,1,512]{2,1,0:T(1,128)} %get-tuple-element.275) | copy-start | bytes 6148
  671.4 23.0 %copy-start.67 = (f32[1,1,512]{2,1,0:T(1,128)S(1)}, f32[1,1,512]{2,1,0:T(1,128)}, u32[]{:S(2)}) copy-start(f32[1,1,512]{2,1,0:T(1,128)} %get-tuple-element.276) | copy-start | bytes 6148
  676.6 27.3 %collective-permute-start.27 = (bf16[256,2,1024]{2,0,1:T(8,128)(2,1)}, bf16[256,2,1024]{2,0,1:T(8,128)(2,1)}, u32[]{:S(2)}, u32[]{:S(2)}) collective-permute-start(bf16[256,2,1024]{2,0,1:T(8,128)(2,1)} %bitcast.371), channel_id=1, source_target_pairs={{0,8},{8,0},{1,9},{9,1},{2,10},{10,2},{3,11},{11,3},{4,12},{12,4},... | collective-permute-start | bytes 3145736 | tf_op jit(solution)/shard_map/ppermute | solution.py:23
  694.3 9.6 %collective-permute-start.25 = (bf16[256,2,1024]{2,0,1:T(8,128)(2,1)S(1)}, bf16[256,2,1024]{2,0,1:T(8,128)(2,1)S(1)}, u32[]{:S(2)}, u32[]{:S(2)}) collective-permute-start(bf16[256,2,1024]{2,0,1:T(8,128)(2,1)S(1)} %bitcast.382), channel_id=1, source_target_pairs={{0,8},{8,0},{1,9},{9,1},{2,10},{10,2},{3,11},{11,3},{4,12},{12,4},... | collective-permute-start | bytes 3145736 | tf_op jit(solution)/shard_map/ppermute | solution.py:23
  (77 other events, 573.5 us)
where the time goes:
time: 729 us; the launch traced here: 721 us
  blocking collectives  294 us (40%)
  starting transfers between devices  117 us (16%)
  other arithmetic  116 us (16%)
  local copies, waits for them, and re-layouts  85.3 us (12%)
  waiting for transfers between devices  76 us (10%)
  matrix products  28.8 us (4%)
    all_gather x1, blocking collectives, reduce_small(): whole = lax.all_gather(mine, axes, axis=0, tiled=True).reshape(-1)  294 us
    all_to_all x2, waiting for transfers between devices, reduce_weights(): pieces = lax.all_to_all(pair, ('dp', *SPACE), 0, 0, tiled=True)  46 us
    ppermute x8, starting transfers between devices, with_halo(): lax.ppermute(lax.slice_in_dim(block, block.shape[dim] - width, None, axis...  32.4 us
    another operation x112, local copies, waits for them, and re-layouts, tap_grads(): rows_out.append(jnp.stack(line))  32.1 us
    reduce_sum x2, other arithmetic, forward_layer(): center = mixed - jnp.mean(mixed, -1, keepdims=True)  27 us
    reduce_sum x9, other arithmetic, tap_grads(): line.append(jnp.sum(window * upstream, axis=(0, 1, 2)))  23.6 us
    ppermute x8, starting transfers between devices, swapped(): return lax.ppermute(value, axis, [(0, 1), (1, 0)])  21.5 us
    ppermute x8, starting transfers between devices, with_halo(): lax.ppermute(lax.slice_in_dim(block, 0, width, axis=dim), axis, backward)  16 us
  transfers between devices with their start and end apart: 33, of which 8 were waited for; matrix products, arithmetic and copies ran while one was open for 22% of the time, Pallas kernels for 0%

commit v1 on v0

--- a/solution.py
+++ b/solution.py
@@ -182,7 +182,9 @@
     lines = jnp.pad(lines, (0, spare)).astype(jnp.bfloat16).reshape(128, -1)
     pieces = lax.all_to_all(lines, axes, 0, 0, tiled=True)
     mine = jnp.sum(pieces.astype(jnp.float32), 0, keepdims=True)
-    whole = lax.all_gather(mine, axes, axis=0, tiled=True).reshape(-1)
+    whole = jnp.concatenate(
+        lax.all_to_all(jnp.stack([mine] * lax.axis_size(axes)), axes, 0, 0), axis=0
+    ).reshape(-1)
     outs = []
     start = 0
     for p in parts:

time: 729 us -> 436 us (0.60)
  blocking collectives: 294 us -> 0 us
    all_gather x1 -> x0, blocking collectives: 294 us -> none  [reduce_small(): whole = lax.all_gather(mine, axes, axis=0, tiled=True).reshape(-1)]
    ppermute x8, starting transfers between devices: 21.5 us -> 6.04 us  [swapped(): return lax.ppermute(value, axis, [(0, 1), (1, 0)])]
    all_to_all x0 -> x1, starting transfers between devices: none -> 10.5 us  [reduce_small(): lax.all_to_all(jnp.stack([mine] * lax.axis_size(axes)), axes, 0, 0)]
  transfers between devices with their start and end apart: 33 -> 34, of which waited for: 8 -> 8; matrix products, arithmetic and copies ran while one was open for 22% -> 39% of each run, Pallas kernels for 0% -> 0%
where the time goes in v1:
time: 436 us; the launch traced here: 427 us
  other arithmetic  117 us (27%)
  starting transfers between devices  112 us (26%)
  local copies, waits for them, and re-layouts  89.8 us (21%)
  waiting for transfers between devices  76.3 us (18%)
  matrix products  28.7 us (7%)
    all_to_all x2, waiting for transfers between devices, reduce_weights(): pieces = lax.all_to_all(pair, ('dp', *SPACE), 0, 0, tiled=True)  46 us
    ppermute x8, starting transfers between devices, with_halo(): lax.ppermute(lax.slice_in_dim(block, block.shape[dim] - width, None, axis...  33 us
    another operation x112, local copies, waits for them, and re-layouts, tap_grads(): rows_out.append(jnp.stack(line))  32.1 us
    reduce_sum x2, other arithmetic, forward_layer(): center = mixed - jnp.mean(mixed, -1, keepdims=True)  27 us
    reduce_sum x9, other arithmetic, tap_grads(): line.append(jnp.sum(window * upstream, axis=(0, 1, 2)))  23.6 us
    ppermute x8, starting transfers between devices, with_halo(): lax.ppermute(lax.slice_in_dim(block, 0, width, axis=dim), axis, backward)  16 us
    all_to_all x2, starting transfers between devices, reduce_weights(): lax.all_to_all(copies, SPACE, 0, 0, tiled=True).reshape(256, 2, HALF)  14.5 us
    all_to_all x2, starting transfers between devices, reduce_weights(): pieces = lax.all_to_all(pair, ('dp', *SPACE), 0, 0, tiled=True)  13.8 us
  transfers between devices with their start and end apart: 34, of which 8 were waited for; matrix products, arithmetic and copies ran while one was open for 39% of the time, Pallas kernels for 0%

profile of v1, /device:TPU:1, one launch (start us, length us, event | category | flops | bytes accessed | tf_op | source)
XLA Modules:
  0.0 427.2 jit_solution(4317246651315442265)
XLA Ops:
  0.7 3.1 fusion.397
  3.8 1.9 dynamic-slice_bitcast_fusion
  5.7 3.3 collective-permute-start.14
  9.0 1.9 dynamic-slice_bitcast_fusion.2
  12.2 4.3 %collective-permute-start = (bf16[1,3,32,512]{3,2,1,0:T(8,128)(2,1)}, bf16[1,3,32,512]{3,2,1,0:T(8,128)(2,1)}, u32[]{:S(2)}, u32[]{:S(2)}) collective-permute-start(bf16[1,3,32,512]{3,2,1,0:T(8,128)(2,1)} %get-tuple-element.217), channel_id=1, source_target_pairs={{0,8},{8,16},{16,24},{24,32},{32,40},{40,48},{48,56},{56,64},{64,7... | collective-permute-start | bytes 294920 | tf_op jit(solution)/shard_map/ppermute | solution.py:57
  16.5 1.9 collective-permute-start.1
  19.9 1.9 dynamic-slice_bitcast_fusion.1
  27.7 1.9 dynamic-slice_bitcast_fusion.3
  36.0 4.2 collective-permute-start.2
  42.4 15.6 %fusion.394 = (f32[16,32]{1,0:T(8,128)S(1)}, f32[1,16,32,512]{3,2,1,0:T(8,128)S(1)}) fusion(f32[512]{0:T(512)} %bitcast.597, f32[512]{0:T(512)S(1)} %bitcast.394, bf16[1,22,3,512]{3,2,1,0:T(4,128)(2,1)} %copy-done.35, bf16[1,22,32,512]{3,2,1,0:T(8,128)(2,1)S(1)} %get-tuple-element.321, f32[512]{0:T(512)S(1)} %bitcast.396, f32[512]{0:T(512)S(1)} %bitcast.398, ...), kind=kLoop, calls=%fused_computation.914 | loop fusion | flops 71826944 | bytes 5679104 | tf_op jit(solution)/shard_map/reduce_sum | solution.py:110
  58.0 3.1 collective-permute-start.13
  66.7 2.5 bitcast_select_fusion.3
  73.5 2.2 bitcast_select_fusion.1
  75.8 2.6 fusion.327
  78.5 2.3 collective-permute-start.9
  80.8 3.3 collective-permute-start.8
  85.8 3.6 collective-permute-start.10
  89.4 1.8 collective-permute-start.11
  91.9 3.0 collective-permute-done.11
  96.7 11.4 %fusion.392 = (f32[16,32]{1,0:T(8,128)S(1)}, f32[1,16,32,512]{3,2,1,0:T(8,128)}) fusion(f32[512]{0:T(512)} %bitcast.601, f32[512]{0:T(512)S(1)} %bitcast.492, bf16[1,22,35,512]{3,2,1,0:T(8,128)(2,1)S(1)} %get-tuple-element.200, f32[512]{0:T(512)S(1)} %bitcast.495, f32[512]{0:T(512)S(1)} %bitcast.497, f32[512]{0:T(512)S(1)} %bitcast.499, ...), kind=kLoop, calls=%fused_computation.913 | loop fusion | flops 40369664 | bytes 23894016 | tf_op jit(solution)/shard_map/reduce_sum | solution.py:110
  111.4 2.8 fusion.24
  114.3 4.2 fusion.416
  118.5 2.1 multiply_reduce_fusion
  121.9 2.0 fusion.15
  124.0 4.3 %fusion.223 = (bf16[512]{0:T(512)(128)(2,1)S(1)}, bf16[512]{0:T(512)(128)(2,1)S(1)}, bf16[512]{0:T(512)(128)(2,1)}, bf16[512]{0:T(512)(128)(2,1)}, bf16[512]{0:T...) fusion(bf16[1,22,35,512]{3,2,1,0:T(8,128)(2,1)S(1)} %get-tuple-, ...), kind=kLoop, calls=%fused_computation.489 | loop fusion | flops 15981568 | bytes 12611584 | tf_op jit(solution)/shard_map/reduce_sum | solution.py:100
  128.3 3.4 fusion.219
  132.4 1.9 collective-permute-start.17
  134.3 5.6 %collective-permute-start.16 = (bf16[1,3,32,512]{3,2,1,0:T(8,128)(2,1)}, bf16[1,3,32,512]{3,2,1,0:T(8,128)(2,1)S(1)}, u32[]{:S(2)}, u32[]{:S(2)}) collective-permute-start(bf16[1,3,32,512]{3,2,1,0:T(8,128)(2,1)} %get-tuple-element.209), channel_id=1, source_target_pairs={{0,8},{8,16},{16,24},{24,32},{32,40},{40,48},{48,56},{56,64},{64,7... | collective-permute-start | bytes 294920 | tf_op jit(solution)/shard_map/ppermute | solution.py:57
  141.5 2.2 fusion.220
  155.6 4.2 collective-permute-start.18
  186.0 10.3 %multiply_reduce_fusion.2 = (bf16[512]{0:T(512)(128)(2,1)}, bf16[512]{0:T(512)(128)(2,1)S(1)}, f32[1,16,32,512]{3,2,1,0:T(8,128)S(1)}) fusion(bf16[1,16,32,512]{3,2,1,0:T(8,128)(2,1)} %param.12, f32[512]{0:T(512)} %bitcast.598, f32[512]{0:T(512)} %bitcast.589, f32[512]{0:T(512)S(1)} %bitcast.491, f32[1,22,38,512]{3,2,1,0:T(8,128)S(1)} %maximum_convert_fusion.2, ...), kind=kLoop, calls=%fused_computation.716 | loop fusion | flops 26999808 | bytes 53059584 | tf_op jit(solution)/shard_map/reduce_sum | solution.py:128
  196.5 3.4 multiply_reduce_fusion.1
  200.0 3.6 fusion.417
  203.6 2.1 multiply_reduce_fusion.3
  207.1 2.0 fusion.13
  219.0 3.7 fusion.121
  222.8 2.9 fusion.123
  225.8 2.0 fusion.125
  228.0 1.9 fusion.120
  229.9 2.2 fusion.124
  235.7 13.6 %all-to-all-start.4 = ((bf16[128,2,256]{2,1,0:T(2,128)(2,1)}), bf16[128,2,256]{2,1,0:T(2,128)(2,1)S(1)}, u32[]{:S(2)}, u32[]{:S(2)}) async-start(bf16[128,2,256]{2,1,0:T(2,128)(2,1)} %reshape.927), calls=%async_computation.4 | async-start | bytes 262144 | tf_op jit(solution)/shard_map/all_to_all | solution.py:183
  249.4 3.1 fusion.17
  254.1 5.1 %all-to-all-done.4 = bf16[128,2,256]{2,1,0:T(2,128)(2,1)S(1)} async-done(((bf16[128,2,256]{2,1,0:T(2,128)(2,1)}), bf16[128,2,256]{2,1,0:T(2,128)(2,1)S(1)}, u32[]{:S(2)}, u32[]{:S(2)}) %all-to-all-start.4) | async-done | bytes 131104 | tf_op jit(solution)/shard_map/all_to_all | solution.py:183
  259.2 5.7 %all-to-all-start.2 = ((bf16[64,8,2,1024]{3,1,2,0:T(8,128)(2,1)}), bf16[64,8,2,1024]{3,1,2,0:T(8,128)(2,1)}, u32[]{:S(2)}, u32[]{:S(2)}) async-start(bf16[64,8,2,1024]{3,1,2,0:T(8,128)(2,1)} %copy.28), calls=%async_computation.2 | async-start | bytes 4194304 | tf_op jit(solution)/shard_map/all_to_all | solution.py:165
  264.9 3.1 fusion.16
  269.6 22.3 %all-to-all-done.2 = bf16[64,8,2,1024]{3,1,2,0:T(8,128)(2,1)} async-done(((bf16[64,8,2,1024]{3,1,2,0:T(8,128)(2,1)}), bf16[64,8,2,1024]{3,1,2,0:T(8,128)(2,1)}, u32[]{:S(2)}, u32[]{:S(2)}) %all-to-all-start.2) | async-done | bytes 2097184 | tf_op jit(solution)/shard_map/all_to_all | solution.py:165
  292.0 8.1 %all-to-all-start = ((bf16[64,8,2,1024]{3,1,2,0:T(8,128)(2,1)}), bf16[64,8,2,1024]{3,1,2,0:T(8,128)(2,1)}, u32[]{:S(2)}, u32[]{:S(2)}) async-start(bf16[64,8,2,1024]{3,1,2,0:T(8,128)(2,1)} %copy.26), calls=%async_computation | async-start | bytes 4194304 | tf_op jit(solution)/shard_map/all_to_all | solution.py:165
  300.1 2.0 reduce_sum.1104
  302.0 23.7 %all-to-all-done = bf16[64,8,2,1024]{3,1,2,0:T(8,128)(2,1)} async-done(((bf16[64,8,2,1024]{3,1,2,0:T(8,128)(2,1)}), bf16[64,8,2,1024]{3,1,2,0:T(8,128)(2,1)}, u32[]{:S(2)}, u32[]{:S(2)}) %all-to-all-start) | async-done | bytes 2097184 | tf_op jit(solution)/shard_map/all_to_all | solution.py:165
  326.8 8.3 %all-to-all-start.3 = ((bf16[32,8,2,1024]{3,1,2,0:T(8,128)(2,1)}), bf16[32,8,2,1024]{3,1,2,0:T(8,128)(2,1)S(1)}, u32[]{:S(2)}, u32[]{:S(2)}) async-start(bf16[32,8,2,1024]{3,1,2,0:T(8,128)(2,1)} %broadcast_in_dim.5), calls=%async_computation.3 | async-start | bytes 2097152 | tf_op jit(solution)/shard_map/all_to_all | solution.py:168
  335.1 2.0 reduce_sum.1103
  337.0 13.6 %all-to-all-done.3 = bf16[32,8,2,1024]{3,1,2,0:T(8,128)(2,1)S(1)} async-done(((bf16[32,8,2,1024]{3,1,2,0:T(8,128)(2,1)}), bf16[32,8,2,1024]{3,1,2,0:T(8,128)(2,1)S(1)}, u32[]{:S(2)}, u32[]{:S(2)}) %all-to-all-start.3) | async-done | bytes 1048608 | tf_op jit(solution)/shard_map/all_to_all | solution.py:168
  351.7 6.2 %all-to-all-start.1 = ((bf16[32,8,2,1024]{3,1,2,0:T(8,128)(2,1)}), bf16[32,8,2,1024]{3,1,2,0:T(8,128)(2,1)}, u32[]{:S(2)}, u32[]{:S(2)}) async-start(bf16[32,8,2,1024]{3,1,2,0:T(8,128)(2,1)} %broadcast_in_dim.4), calls=%async_computation.1 | async-start | bytes 2097152 | tf_op jit(solution)/shard_map/all_to_all | solution.py:168
  358.0 4.2 collective-permute-start.21
  362.2 3.2 collective-permute-start.20
  365.5 6.7 %collective-permute-done.21 = bf16[1,3,32,512]{3,2,1,0:T(8,128)(2,1)S(1)} collective-permute-done((bf16[1,3,32,512]{3,2,1,0:T(8,128)(2,1)S(1)}, bf16[1,3,32,512]{3,2,1,0:T(8,128)(2,1)S(1)}, u32[]{:S(2)}, u32[]{:S(2)}) %collective-permute-start.21) | collective-permute-done | bytes 98336 | tf_op jit(solution)/shard_map/ppermute | solution.py:60
  373.7 4.6 %collective-permute-start.22 = (bf16[1,22,3,512]{3,2,1,0:T(4,128)(2,1)S(1)}, bf16[1,22,3,512]{3,2,1,0:T(4,128)(2,1)}, u32[]{:S(2)}, u32[]{:S(2)}) collective-permute-start(bf16[1,22,3,512]{3,2,1,0:T(4,128)(2,1)S(1)} %get-tuple-element.195), channel_id=1, source_target_pairs={{0,2},{2,4},{4,6},{1,3},{3,5},{5,7},{8,10},{10,12},{12,14},{9,11},... | collective-permute-start | bytes 202760 | tf_op jit(solution)/shard_map/ppermute | solution.py:57
  383.9 10.5 %all-to-all-start.5 = ((f32[128,1,512]{2,1,0:T(1,128)}), f32[128,1,512]{2,1,0:T(1,128)S(1)}, u32[]{:S(2)}, u32[]{:S(2)}) async-start(f32[128,1,512]{2,1,0:T(1,128)} %stack.794), calls=%async_computation.5 | async-start | bytes 524288 | tf_op jit(solution)/shard_map/all_to_all | solution.py:186
  394.4 2.3 copy.52
  397.9 9.3 %fusion.226 = bf16[1,16,32,512]{3,2,1,0:T(8,128)(2,1)} fusion(f32[1,22,38,512]{3,2,1,0:T(8,128)S(1)} %maximum_convert_fusion.3, f32[1,16,32,512]{3,2,1,0:T(8,128)} %copy-done.22, bf16[1,16,32,512]{3,2,1,0:T(8,128)(2,1)} %param.12, f32[512]{0:T(512)S(1)} %bitcast.395, f32[512]{0:T(512)S(1)} %bitcast.397, f32[512]{0:T(512)S(1)} %bitcast.399, ...), kind=kLoop, calls=%fused_computation.493 | loop fusion | flops 26476544 | bytes 53577728 | tf_op jit(solution)/shard_map/convert_element_type | solution.py:258
  410.0 2.1 broadcast_select_fusion.1
  415.4 2.3 pad_maximum_fusion.1
  417.7 5.3 %copy.31 = f32[2,2048,256]{2,1,0:T(8,128)} copy(f32[2,2048,256]{1,2,0:T(8,128)} %pad_maximum_fusion.1) | data formatting | bytes 8388608
  423.0 4.0 pad_maximum_fusion
  (511 shorter events, 109.9 us)
Async XLA Ops:
  3.8 22.1 %copy-start.112 = (f32[2,512]{1,0:T(2,128)S(1)}, f32[2,512]{1,0:T(2,128)}, u32[]{:S(2)}) copy-start(f32[2,512]{1,0:T(2,128)} %param.21) | copy-start | bytes 12292
  3.8 22.7 %copy-start.113 = (f32[2,512]{1,0:T(2,128)S(1)}, f32[2,512]{1,0:T(2,128)}, u32[]{:S(2)}) copy-start(f32[2,512]{1,0:T(2,128)} %param.20) | copy-start | bytes 12292
  3.8 23.3 %copy-start.114 = (f32[2,512]{1,0:T(2,128)S(1)}, f32[2,512]{1,0:T(2,128)}, u32[]{:S(2)}) copy-start(f32[2,512]{1,0:T(2,128)} %param.14) | copy-start | bytes 12292
  5.7 57.6 %collective-permute-start.14 = (bf16[1024,256]{1,0:T(8,128)(2,1)}, bf16[1024,256]{1,0:T(8,128)(2,1)}, u32[]{:S(2)}, u32[]{:S(2)}) collective-permute-start(bf16[1024,256]{1,0:T(8,128)(2,1)} %dynamic-slice_bitcast_fusion), channel_id=1, source_target_pairs={{0,65},{1,0},{64,1},{65,64},{2,67},{3,2},{66,3},{67,66},{4,69},{5,... | collective-permute-start | bytes 1572872 | tf_op jit(solution)/shard_map/ppermute | solution.py:32
  9.0 20.6 %copy-start.95 = (f32[2,2048]{1,0:T(2,128)S(1)}, f32[2,2048]{1,0:T(2,128)}, u32[]{:S(2)}) copy-start(f32[2,2048]{1,0:T(2,128)} %param.18) | copy-start | bytes 49156
  10.9 52.9 %collective-permute-start.6 = (bf16[1024,256]{1,0:T(8,128)(2,1)}, bf16[1024,256]{1,0:T(8,128)(2,1)}, u32[]{:S(2)}, u32[]{:S(2)}) collective-permute-start(bf16[1024,256]{1,0:T(8,128)(2,1)} %dynamic-slice_bitcast_fusion.2), channel_id=1, source_target_pairs={{0,65},{1,0},{64,1},{65,64},{2,67},{3,2},{66,3},{67,66},{4,69},{5,... | collective-permute-start | bytes 1572872 | tf_op jit(solution)/shard_map/ppermute | solution.py:32
  12.2 20.3 %collective-permute-start = (bf16[1,3,32,512]{3,2,1,0:T(8,128)(2,1)}, bf16[1,3,32,512]{3,2,1,0:T(8,128)(2,1)}, u32[]{:S(2)}, u32[]{:S(2)}) collective-permute-start(bf16[1,3,32,512]{3,2,1,0:T(8,128)(2,1)} %get-tuple-element.217), channel_id=1, source_target_pairs={{0,8},{8,16},{16,24},{24,32},{32,40},{40,48},{48,56},{56,64},{64,7... | collective-permute-start | bytes 294920 | tf_op jit(solution)/shard_map/ppermute | solution.py:57
  16.5 17.0 %collective-permute-start.1 = (bf16[1,3,32,512]{3,2,1,0:T(8,128)(2,1)}, bf16[1,3,32,512]{3,2,1,0:T(8,128)(2,1)}, u32[]{:S(2)}, u32[]{:S(2)}) collective-permute-start(bf16[1,3,32,512]{3,2,1,0:T(8,128)(2,1)} %get-tuple-element.216), channel_id=1, source_target_pairs={{8,0},{16,8},{24,16},{32,24},{40,32},{48,40},{56,48},{64,56},{72,6... | collective-permute-start | bytes 294920 | tf_op jit(solution)/shard_map/ppermute | solution.py:60
  21.8 36.2 %collective-permute-start.12 = (bf16[128,2048]{1,0:T(8,128)(2,1)}, bf16[128,2048]{1,0:T(8,128)(2,1)}, u32[]{:S(2)}, u32[]{:S(2)}) collective-permute-start(bf16[128,2048]{1,0:T(8,128)(2,1)} %dynamic-slice_bitcast_fusion.1), channel_id=1, source_target_pairs={{0,1},{1,64},{64,65},{65,0},{2,3},{3,66},{66,67},{67,2},{4,5},{5,6... | collective-permute-start | bytes 1572872 | tf_op jit(solution)/shard_map/ppermute | solution.py:31
  24.6 33.3 %copy-start.56 = (f32[1,1,512]{2,1,0:T(1,128)}, f32[1,1,512]{2,1,0:T(1,128)S(1)}, u32[]{:S(2)}) copy-start(f32[1,1,512]{2,1,0:T(1,128)S(1)} %get-tuple-element.269) | copy-start | bytes 6148
  24.6 33.3 %copy-start.58 = (f32[1,1,512]{2,1,0:T(1,128)}, f32[1,1,512]{2,1,0:T(1,128)S(1)}, u32[]{:S(2)}) copy-start(f32[1,1,512]{2,1,0:T(1,128)S(1)} %get-tuple-element.270) | copy-start | bytes 6148
  24.6 33.3 %copy-start.60 = (f32[1,1,512]{2,1,0:T(1,128)}, f32[1,1,512]{2,1,0:T(1,128)S(1)}, u32[]{:S(2)}) copy-start(f32[1,1,512]{2,1,0:T(1,128)S(1)} %get-tuple-element.271) | copy-start | bytes 6148
  24.6 33.3 %copy-start.62 = (f32[1,1,512]{2,1,0:T(1,128)}, f32[1,1,512]{2,1,0:T(1,128)S(1)}, u32[]{:S(2)}) copy-start(f32[1,1,512]{2,1,0:T(1,128)S(1)} %get-tuple-element.272) | copy-start | bytes 6148
  33.5 29.8 %copy-start = (bf16[1,19,32,512]{3,2,1,0:T(8,128)(2,1)}, bf16[1,19,32,512]{3,2,1,0:T(8,128)(2,1)S(1)}, u32[]{:S(2)}) copy-start(bf16[1,19,32,512]{3,2,1,0:T(8,128)(2,1)S(1)} %get-tuple-element.213) | copy-start | bytes 1867780
  34.7 6.1 %collective-permute-start.3 = (bf16[1,22,3,512]{3,2,1,0:T(4,128)(2,1)S(1)}, bf16[1,22,3,512]{3,2,1,0:T(4,128)(2,1)S(1)}, u32[]{:S(2)}, u32[]{:S(2)}) collective-permute-start(bf16[1,22,3,512]{3,2,1,0:T(4,128)(2,1)S(1)} %get-tuple-element.204), channel_id=1, source_target_pairs={{2,0},{4,2},{6,4},{3,1},{5,3},{7,5},{10,8},{12,10},{14,12},{11,9},... | collective-permute-start | bytes 202760 | tf_op jit(solution)/shard_map/ppermute | solution.py:60
  36.0 5.7 %collective-permute-start.2 = (bf16[1,22,3,512]{3,2,1,0:T(4,128)(2,1)S(1)}, bf16[1,22,3,512]{3,2,1,0:T(4,128)(2,1)S(1)}, u32[]{:S(2)}, u32[]{:S(2)}) collective-permute-start(bf16[1,22,3,512]{3,2,1,0:T(4,128)(2,1)S(1)} %get-tuple-element.203), channel_id=1, source_target_pairs={{0,2},{2,4},{4,6},{1,3},{3,5},{5,7},{8,10},{10,12},{12,14},{9,11},... | collective-permute-start | bytes 202760 | tf_op jit(solution)/shard_map/ppermute | solution.py:57
  40.8 21.4 %collective-permute-start.4 = (bf16[128,2048]{1,0:T(8,128)(2,1)}, bf16[128,2048]{1,0:T(8,128)(2,1)}, u32[]{:S(2)}, u32[]{:S(2)}) collective-permute-start(bf16[128,2048]{1,0:T(8,128)(2,1)} %dynamic-slice_bitcast_fusion.3), channel_id=1, source_target_pairs={{0,1},{1,64},{64,65},{65,0},{2,3},{3,66},{66,67},{67,2},{4,5},{5,6... | collective-permute-start | bytes 1572872 | tf_op jit(solution)/shard_map/ppermute | solution.py:31
  58.0 6.2 %collective-permute-start.13 = (bf16[128,2048]{1,0:T(8,128)(2,1)}, bf16[128,2048]{1,0:T(8,128)(2,1)}, u32[]{:S(2)}, u32[]{:S(2)}) collective-permute-start(bf16[128,2048]{1,0:T(8,128)(2,1)} %collective-permute-done.12), channel_id=1, source_target_pairs={{0,8},{8,0},{1,9},{9,1},{2,10},{10,2},{3,11},{11,3},{4,12},{12,4},... | collective-permute-start | bytes 1572872 | tf_op jit(solution)/shard_map/ppermute | solution.py:23
  62.2 3.4 collective-permute-start.5
  63.3 5.8 %collective-permute-start.15 = (bf16[1024,256]{1,0:T(8,128)(2,1)}, bf16[1024,256]{1,0:T(8,128)(2,1)S(1)}, u32[]{:S(2)}, u32[]{:S(2)}) collective-permute-start(bf16[1024,256]{1,0:T(8,128)(2,1)} %collective-permute-done.14), channel_id=1, source_target_pairs={{0,8},{8,0},{1,9},{9,1},{2,10},{10,2},{3,11},{11,3},{4,12},{12,4},... | collective-permute-start | bytes 1572872 | tf_op jit(solution)/shard_map/ppermute | solution.py:23
  63.8 8.1 %collective-permute-start.7 = (bf16[1024,256]{1,0:T(8,128)(2,1)}, bf16[1024,256]{1,0:T(8,128)(2,1)S(1)}, u32[]{:S(2)}, u32[]{:S(2)}) collective-permute-start(bf16[1024,256]{1,0:T(8,128)(2,1)} %collective-permute-done.6), channel_id=1, source_target_pairs={{0,8},{8,0},{1,9},{9,1},{2,10},{10,2},{3,11},{11,3},{4,12},{12,4},... | collective-permute-start | bytes 1572872 | tf_op jit(solution)/shard_map/ppermute | solution.py:23
  78.5 6.3 %collective-permute-start.9 = (bf16[1,3,32,512]{3,2,1,0:T(8,128)(2,1)S(1)}, bf16[1,3,32,512]{3,2,1,0:T(8,128)(2,1)S(1)}, u32[]{:S(2)}, u32[]{:S(2)}) collective-permute-start(bf16[1,3,32,512]{3,2,1,0:T(8,128)(2,1)S(1)} %get-tuple-element.212), channel_id=1, source_target_pairs={{8,0},{16,8},{24,16},{32,24},{40,32},{48,40},{56,48},{64,56},{72,6... | collective-permute-start | bytes 294920 | tf_op jit(solution)/shard_map/ppermute | solution.py:60
  80.8 4.9 %collective-permute-start.8 = (bf16[1,3,32,512]{3,2,1,0:T(8,128)(2,1)S(1)}, bf16[1,3,32,512]{3,2,1,0:T(8,128)(2,1)S(1)}, u32[]{:S(2)}, u32[]{:S(2)}) collective-permute-start(bf16[1,3,32,512]{3,2,1,0:T(8,128)(2,1)S(1)} %get-tuple-element.211), channel_id=1, source_target_pairs={{0,8},{8,16},{16,24},{24,32},{32,40},{40,48},{48,56},{56,64},{64,7... | collective-permute-start | bytes 294920 | tf_op jit(solution)/shard_map/ppermute | solution.py:57
  85.8 6.1 %collective-permute-start.10 = (bf16[1,22,3,512]{3,2,1,0:T(4,128)(2,1)S(1)}, bf16[1,22,3,512]{3,2,1,0:T(4,128)(2,1)S(1)}, u32[]{:S(2)}, u32[]{:S(2)}) collective-permute-start(bf16[1,22,3,512]{3,2,1,0:T(4,128)(2,1)S(1)} %get-tuple-element.201), channel_id=1, source_target_pairs={{0,2},{2,4},{4,6},{1,3},{3,5},{5,7},{8,10},{10,12},{12,14},{9,11},... | collective-permute-start | bytes 202760 | tf_op jit(solution)/shard_map/ppermute | solution.py:57
  89.4 5.5 %collective-permute-start.11 = (bf16[1,22,3,512]{3,2,1,0:T(4,128)(2,1)S(1)}, bf16[1,22,3,512]{3,2,1,0:T(4,128)(2,1)S(1)}, u32[]{:S(2)}, u32[]{:S(2)}) collective-permute-start(bf16[1,22,3,512]{3,2,1,0:T(4,128)(2,1)S(1)} %get-tuple-element.202), channel_id=1, source_target_pairs={{2,0},{4,2},{6,4},{3,1},{5,3},{7,5},{10,8},{12,10},{14,12},{11,9},... | collective-permute-start | bytes 202760 | tf_op jit(solution)/shard_map/ppermute | solution.py:60
  132.4 20.8 %collective-permute-start.17 = (bf16[1,3,32,512]{3,2,1,0:T(8,128)(2,1)}, bf16[1,3,32,512]{3,2,1,0:T(8,128)(2,1)S(1)}, u32[]{:S(2)}, u32[]{:S(2)}) collective-permute-start(bf16[1,3,32,512]{3,2,1,0:T(8,128)(2,1)} %get-tuple-element.210), channel_id=1, source_target_pairs={{8,0},{16,8},{24,16},{32,24},{40,32},{48,40},{56,48},{64,56},{72,6... | collective-permute-start | bytes 294920 | tf_op jit(solution)/shard_map/ppermute | solution.py:60
  134.3 18.9 %collective-permute-start.16 = (bf16[1,3,32,512]{3,2,1,0:T(8,128)(2,1)}, bf16[1,3,32,512]{3,2,1,0:T(8,128)(2,1)S(1)}, u32[]{:S(2)}, u32[]{:S(2)}) collective-permute-start(bf16[1,3,32,512]{3,2,1,0:T(8,128)(2,1)} %get-tuple-element.209), channel_id=1, source_target_pairs={{0,8},{8,16},{16,24},{24,32},{32,40},{40,48},{48,56},{56,64},{64,7... | collective-permute-start | bytes 294920 | tf_op jit(solution)/shard_map/ppermute | solution.py:57
  141.5 107.9 %collective-permute-start.26 = (bf16[512,2,1024]{2,0,1:T(8,128)(2,1)}, bf16[512,2,1024]{2,0,1:T(8,128)(2,1)}, u32[]{:S(2)}, u32[]{:S(2)}) collective-permute-start(bf16[512,2,1024]{2,0,1:T(8,128)(2,1)} %fusion.18), channel_id=1, source_target_pairs={{0,8},{8,0},{1,9},{9,1},{2,10},{10,2},{3,11},{11,3},{4,12},{12,4},... | collective-permute-start | bytes 6291464 | tf_op jit(solution)/shard_map/ppermute | solution.py:23
  154.3 30.3 %collective-permute-start.19 = (bf16[1,22,3,512]{3,2,1,0:T(4,128)(2,1)S(1)}, bf16[1,22,3,512]{3,2,1,0:T(4,128)(2,1)S(1)}, u32[]{:S(2)}, u32[]{:S(2)}) collective-permute-start(bf16[1,22,3,512]{3,2,1,0:T(4,128)(2,1)S(1)} %get-tuple-element.198), channel_id=1, source_target_pairs={{2,0},{4,2},{6,4},{3,1},{5,3},{7,5},{10,8},{12,10},{14,12},{11,9},... | collective-permute-start | bytes 202760 | tf_op jit(solution)/shard_map/ppermute | solution.py:60
  155.6 29.0 %collective-permute-start.18 = (bf16[1,22,3,512]{3,2,1,0:T(4,128)(2,1)S(1)}, bf16[1,22,3,512]{3,2,1,0:T(4,128)(2,1)S(1)}, u32[]{:S(2)}, u32[]{:S(2)}) collective-permute-start(bf16[1,22,3,512]{3,2,1,0:T(4,128)(2,1)S(1)} %get-tuple-element.197), channel_id=1, source_target_pairs={{0,2},{2,4},{4,6},{1,3},{3,5},{5,7},{8,10},{10,12},{12,14},{9,11},... | collective-permute-start | bytes 202760 | tf_op jit(solution)/shard_map/ppermute | solution.py:57
  159.8 36.6 %copy-start.52 = (bf16[7,7,512]{2,1,0:T(8,128)(2,1)}, bf16[7,7,512]{2,1,0:T(8,128)(2,1)S(1)}, u32[]{:S(2)}) copy-start(bf16[7,7,512]{2,1,0:T(8,128)(2,1)S(1)} %constant_dynamic-update-slice_fusion.18) | copy-start | bytes 150532
  210.8 54.1 %collective-permute-start.24 = (bf16[512,2,1024]{2,0,1:T(8,128)(2,1)}, bf16[512,2,1024]{2,0,1:T(8,128)(2,1)}, u32[]{:S(2)}, u32[]{:S(2)}) collective-permute-start(bf16[512,2,1024]{2,0,1:T(8,128)(2,1)} %fusion.20), channel_id=1, source_target_pairs={{0,8},{8,0},{1,9},{9,1},{2,10},{10,2},{3,11},{11,3},{4,12},{12,4},... | collective-permute-start | bytes 6291464 | tf_op jit(solution)/shard_map/ppermute | solution.py:23
  235.7 23.5 %all-to-all-start.4 = ((bf16[128,2,256]{2,1,0:T(2,128)(2,1)}), bf16[128,2,256]{2,1,0:T(2,128)(2,1)S(1)}, u32[]{:S(2)}, u32[]{:S(2)}) async-start(bf16[128,2,256]{2,1,0:T(2,128)(2,1)} %reshape.927), calls=%async_computation.4 | async-start | bytes 262144 | tf_op jit(solution)/shard_map/all_to_all | solution.py:183
  259.2 32.8 %all-to-all-start.2 = ((bf16[64,8,2,1024]{3,1,2,0:T(8,128)(2,1)}), bf16[64,8,2,1024]{3,1,2,0:T(8,128)(2,1)}, u32[]{:S(2)}, u32[]{:S(2)}) async-start(bf16[64,8,2,1024]{3,1,2,0:T(8,128)(2,1)} %copy.28), calls=%async_computation.2 | async-start | bytes 4194304 | tf_op jit(solution)/shard_map/all_to_all | solution.py:165
  292.0 33.7 %all-to-all-start = ((bf16[64,8,2,1024]{3,1,2,0:T(8,128)(2,1)}), bf16[64,8,2,1024]{3,1,2,0:T(8,128)(2,1)}, u32[]{:S(2)}, u32[]{:S(2)}) async-start(bf16[64,8,2,1024]{3,1,2,0:T(8,128)(2,1)} %copy.26), calls=%async_computation | async-start | bytes 4194304 | tf_op jit(solution)/shard_map/all_to_all | solution.py:165
  326.8 23.8 %all-to-all-start.3 = ((bf16[32,8,2,1024]{3,1,2,0:T(8,128)(2,1)}), bf16[32,8,2,1024]{3,1,2,0:T(8,128)(2,1)S(1)}, u32[]{:S(2)}, u32[]{:S(2)}) async-start(bf16[32,8,2,1024]{3,1,2,0:T(8,128)(2,1)} %broadcast_in_dim.5), calls=%async_computation.3 | async-start | bytes 2097152 | tf_op jit(solution)/shard_map/all_to_all | solution.py:168
  351.7 30.7 %all-to-all-start.1 = ((bf16[32,8,2,1024]{3,1,2,0:T(8,128)(2,1)}), bf16[32,8,2,1024]{3,1,2,0:T(8,128)(2,1)}, u32[]{:S(2)}, u32[]{:S(2)}) async-start(bf16[32,8,2,1024]{3,1,2,0:T(8,128)(2,1)} %broadcast_in_dim.4), calls=%async_computation.1 | async-start | bytes 2097152 | tf_op jit(solution)/shard_map/all_to_all | solution.py:168
  358.0 14.1 %collective-permute-start.21 = (bf16[1,3,32,512]{3,2,1,0:T(8,128)(2,1)S(1)}, bf16[1,3,32,512]{3,2,1,0:T(8,128)(2,1)S(1)}, u32[]{:S(2)}, u32[]{:S(2)}) collective-permute-start(bf16[1,3,32,512]{3,2,1,0:T(8,128)(2,1)S(1)} %get-tuple-element.208), channel_id=1, source_target_pairs={{8,0},{16,8},{24,16},{32,24},{40,32},{48,40},{56,48},{64,56},{72,6... | collective-permute-start | bytes 294920 | tf_op jit(solution)/shard_map/ppermute | solution.py:60
  362.2 9.9 %collective-permute-start.20 = (bf16[1,3,32,512]{3,2,1,0:T(8,128)(2,1)S(1)}, bf16[1,3,32,512]{3,2,1,0:T(8,128)(2,1)S(1)}, u32[]{:S(2)}, u32[]{:S(2)}) collective-permute-start(bf16[1,3,32,512]{3,2,1,0:T(8,128)(2,1)S(1)} %get-tuple-element.207), channel_id=1, source_target_pairs={{0,8},{8,16},{16,24},{24,32},{32,40},{40,48},{48,56},{56,64},{64,7... | collective-permute-start | bytes 294920 | tf_op jit(solution)/shard_map/ppermute | solution.py:57
  372.2 25.5 %copy-start.57 = (f32[1,1,512]{2,1,0:T(1,128)S(1)}, f32[1,1,512]{2,1,0:T(1,128)}, u32[]{:S(2)}) copy-start(f32[1,1,512]{2,1,0:T(1,128)} %copy-done.56) | copy-start | bytes 6148
  372.2 25.5 %copy-start.59 = (f32[1,1,512]{2,1,0:T(1,128)S(1)}, f32[1,1,512]{2,1,0:T(1,128)}, u32[]{:S(2)}) copy-start(f32[1,1,512]{2,1,0:T(1,128)} %copy-done.58) | copy-start | bytes 6148
  372.2 25.5 %copy-start.61 = (f32[1,1,512]{2,1,0:T(1,128)S(1)}, f32[1,1,512]{2,1,0:T(1,128)}, u32[]{:S(2)}) copy-start(f32[1,1,512]{2,1,0:T(1,128)} %copy-done.60) | copy-start | bytes 6148
  372.2 25.5 %copy-start.63 = (f32[1,1,512]{2,1,0:T(1,128)S(1)}, f32[1,1,512]{2,1,0:T(1,128)}, u32[]{:S(2)}) copy-start(f32[1,1,512]{2,1,0:T(1,128)} %copy-done.62) | copy-start | bytes 6148
  372.2 25.5 %copy-start.64 = (f32[1,1,512]{2,1,0:T(1,128)S(1)}, f32[1,1,512]{2,1,0:T(1,128)}, u32[]{:S(2)}) copy-start(f32[1,1,512]{2,1,0:T(1,128)} %get-tuple-element.273) | copy-start | bytes 6148
  372.3 25.5 %copy-start.65 = (f32[1,1,512]{2,1,0:T(1,128)S(1)}, f32[1,1,512]{2,1,0:T(1,128)}, u32[]{:S(2)}) copy-start(f32[1,1,512]{2,1,0:T(1,128)} %get-tuple-element.274) | copy-start | bytes 6148
  372.3 25.5 %copy-start.66 = (f32[1,1,512]{2,1,0:T(1,128)S(1)}, f32[1,1,512]{2,1,0:T(1,128)}, u32[]{:S(2)}) copy-start(f32[1,1,512]{2,1,0:T(1,128)} %get-tuple-element.275) | copy-start | bytes 6148
  372.3 25.5 %copy-start.67 = (f32[1,1,512]{2,1,0:T(1,128)S(1)}, f32[1,1,512]{2,1,0:T(1,128)}, u32[]{:S(2)}) copy-start(f32[1,1,512]{2,1,0:T(1,128)} %get-tuple-element.276) | copy-start | bytes 6148
  372.3 25.5 %copy-start.68 = (f32[1,1,512]{2,1,0:T(1,128)S(1)}, f32[1,1,512]{2,1,0:T(1,128)}, u32[]{:S(2)}) copy-start(f32[1,1,512]{2,1,0:T(1,128)} %get-tuple-element.277) | copy-start | bytes 6148
  372.3 25.5 %copy-start.69 = (f32[1,1,512]{2,1,0:T(1,128)S(1)}, f32[1,1,512]{2,1,0:T(1,128)}, u32[]{:S(2)}) copy-start(f32[1,1,512]{2,1,0:T(1,128)} %get-tuple-element.278) | copy-start | bytes 6148
  372.3 25.5 %copy-start.70 = (f32[1,1,512]{2,1,0:T(1,128)S(1)}, f32[1,1,512]{2,1,0:T(1,128)}, u32[]{:S(2)}) copy-start(f32[1,1,512]{2,1,0:T(1,128)} %get-tuple-element.279) | copy-start | bytes 6148
  372.3 25.5 %copy-start.71 = (f32[1,1,512]{2,1,0:T(1,128)S(1)}, f32[1,1,512]{2,1,0:T(1,128)}, u32[]{:S(2)}) copy-start(f32[1,1,512]{2,1,0:T(1,128)} %get-tuple-element.280) | copy-start | bytes 6148
  372.3 25.5 %copy-start.72 = (f32[1,1,512]{2,1,0:T(1,128)S(1)}, f32[1,1,512]{2,1,0:T(1,128)}, u32[]{:S(2)}) copy-start(f32[1,1,512]{2,1,0:T(1,128)} %get-tuple-element.281) | copy-start | bytes 6148
  372.3 25.5 %copy-start.73 = (f32[1,1,512]{2,1,0:T(1,128)S(1)}, f32[1,1,512]{2,1,0:T(1,128)}, u32[]{:S(2)}) copy-start(f32[1,1,512]{2,1,0:T(1,128)} %get-tuple-element.282) | copy-start | bytes 6148
  372.3 25.5 %copy-start.74 = (f32[1,1,512]{2,1,0:T(1,128)S(1)}, f32[1,1,512]{2,1,0:T(1,128)}, u32[]{:S(2)}) copy-start(f32[1,1,512]{2,1,0:T(1,128)} %get-tuple-element.283) | copy-start | bytes 6148
  372.4 25.5 %copy-start.75 = (f32[1,1,512]{2,1,0:T(1,128)S(1)}, f32[1,1,512]{2,1,0:T(1,128)}, u32[]{:S(2)}) copy-start(f32[1,1,512]{2,1,0:T(1,128)} %get-tuple-element.284) | copy-start | bytes 6148
  372.4 25.5 %copy-start.76 = (f32[1,1,512]{2,1,0:T(1,128)S(1)}, f32[1,1,512]{2,1,0:T(1,128)}, u32[]{:S(2)}) copy-start(f32[1,1,512]{2,1,0:T(1,128)} %get-tuple-element.285) | copy-start | bytes 6148
  372.4 25.5 %copy-start.77 = (f32[1,1,512]{2,1,0:T(1,128)S(1)}, f32[1,1,512]{2,1,0:T(1,128)}, u32[]{:S(2)}) copy-start(f32[1,1,512]{2,1,0:T(1,128)} %get-tuple-element.286) | copy-start | bytes 6148
  372.4 25.5 %copy-start.78 = (f32[1,1,512]{2,1,0:T(1,128)S(1)}, f32[1,1,512]{2,1,0:T(1,128)}, u32[]{:S(2)}) copy-start(f32[1,1,512]{2,1,0:T(1,128)} %get-tuple-element.287) | copy-start | bytes 6148
  372.4 25.5 %copy-start.79 = (f32[1,1,512]{2,1,0:T(1,128)S(1)}, f32[1,1,512]{2,1,0:T(1,128)}, u32[]{:S(2)}) copy-start(f32[1,1,512]{2,1,0:T(1,128)} %get-tuple-element.288) | copy-start | bytes 6148
  372.4 6.9 %collective-permute-start.23 = (bf16[1,22,3,512]{3,2,1,0:T(4,128)(2,1)S(1)}, bf16[1,22,3,512]{3,2,1,0:T(4,128)(2,1)S(1)}, u32[]{:S(2)}, u32[]{:S(2)}) collective-permute-start(bf16[1,22,3,512]{3,2,1,0:T(4,128)(2,1)S(1)} %get-tuple-element.196), channel_id=1, source_target_pairs={{2,0},{4,2},{6,4},{3,1},{5,3},{7,5},{10,8},{12,10},{14,12},{11,9},... | collective-permute-start | bytes 202760 | tf_op jit(solution)/shard_map/ppermute | solution.py:60
  373.7 6.3 %collective-permute-start.22 = (bf16[1,22,3,512]{3,2,1,0:T(4,128)(2,1)S(1)}, bf16[1,22,3,512]{3,2,1,0:T(4,128)(2,1)}, u32[]{:S(2)}, u32[]{:S(2)}) collective-permute-start(bf16[1,22,3,512]{3,2,1,0:T(4,128)(2,1)S(1)} %get-tuple-element.195), channel_id=1, source_target_pairs={{0,2},{2,4},{4,6},{1,3},{3,5},{5,7},{8,10},{10,12},{12,14},{9,11},... | collective-permute-start | bytes 202760 | tf_op jit(solution)/shard_map/ppermute | solution.py:57
  382.4 27.6 %collective-permute-start.27 = (bf16[256,2,1024]{2,0,1:T(8,128)(2,1)}, bf16[256,2,1024]{2,0,1:T(8,128)(2,1)}, u32[]{:S(2)}, u32[]{:S(2)}) collective-permute-start(bf16[256,2,1024]{2,0,1:T(8,128)(2,1)} %bitcast.370), channel_id=1, source_target_pairs={{0,8},{8,0},{1,9},{9,1},{2,10},{10,2},{3,11},{11,3},{4,12},{12,4},... | collective-permute-start | bytes 3145736 | tf_op jit(solution)/shard_map/ppermute | solution.py:23
  383.9 23.3 %all-to-all-start.5 = ((f32[128,1,512]{2,1,0:T(1,128)}), f32[128,1,512]{2,1,0:T(1,128)S(1)}, u32[]{:S(2)}, u32[]{:S(2)}) async-start(f32[128,1,512]{2,1,0:T(1,128)} %stack.794), calls=%async_computation.5 | async-start | bytes 524288 | tf_op jit(solution)/shard_map/all_to_all | solution.py:186
  396.7 13.3 %collective-permute-start.25 = (bf16[256,2,1024]{2,0,1:T(8,128)(2,1)}, bf16[256,2,1024]{2,0,1:T(8,128)(2,1)}, u32[]{:S(2)}, u32[]{:S(2)}) collective-permute-start(bf16[256,2,1024]{2,0,1:T(8,128)(2,1)} %bitcast.371), channel_id=1, source_target_pairs={{0,8},{8,0},{1,9},{9,1},{2,10},{10,2},{3,11},{11,3},{4,12},{12,4},... | collective-permute-start | bytes 3145736 | tf_op jit(solution)/shard_map/ppermute | solution.py:23
  (90 other events, 790.3 us)
